TPU v7x, 32 devices: a whole 2x2x4 slice. The times are simulated.
32 devices in a mesh: groups: 2 (over y), users: 4 (over z), routers: 2 (over x), heads: 2 (over core).
Axes of the slice: x: 2, y: 2, z: 4, core: 2. Of those that a mesh axis runs over, the one named last changes fastest.
Arguments:
- items: bfloat16 [64, 64, 1024], P(('groups', 'users', 'routers')), parts along dimension 0, may hold values from -6 to 6
- block_owner: int32 [64, 1], P(('groups', 'users', 'routers')), parts along dimension 0, may hold values from 0 to 3; in each aligned block of 4 rows (0 to 3, 4 to 7, ...) at most 2 rows name the same one
- block_user: int32 [64], P(('groups', 'users', 'routers')), parts along dimension 0, may hold values from 0 to 1
- block_fill: int32 [64], P(('groups', 'users', 'routers')), parts along dimension 0, may hold values from 1 to 64
- prefix_keys: bfloat16 [16, 256, 1024], P(('groups', 'users'), None, 'heads'), parts along dimension 0, may hold values from -6 to 6
- prefix_values: bfloat16 [16, 256, 1024], P(('groups', 'users'), None, 'heads'), parts along dimension 0, may hold values from -6 to 6
- w_in: bfloat16 [4, 1024, 1024], P(None, 'routers', 'heads'), may hold values from -0.1875 to 0.1875
- attn_gain: bfloat16 [1024], P('heads'), may hold values from 0.25 to 1.75
- w_o: bfloat16 [1024, 1024], P('heads', 'routers'), may hold values from -0.1875 to 0.1875
- mlp_gain: bfloat16 [1024], replicated, may hold values from 0.25 to 1.75
- w_one: bfloat16 [1024, 256], replicated, may hold values from -0.1875 to 0.1875
- w_two: bfloat16 [256], replicated, may hold values from -0.375 to 0.375
Outputs:
- scores: float32 [64, 64], P(('groups', 'users', 'routers')), parts along dimension 0
There are 2 independent parts, one for each index of `groups`. A program takes and returns all parts, laid end to end along the dimension named above; an argument that names none is the same for every part. Nothing has to cross between parts.
Inputs may be any that keep to these rules, and one draw needn't show every extreme that they name: `block_owner`: within the rows of one device (aligned blocks of 4 blocks), no owner is named by more than 2 rows, and in every draw some owner is named by exactly 2 rows of some device.
All inputs are finite; a program needn't handle non-finite values.
Results may differ from a plain program's by a relative error of at most 0.005.
Values may be sent and summed in bfloat16 or wider, within the bound.
A program may use at most 64 MiB of HBM per device.

v0:
```python
import jax
import jax.numpy as jnp
from jax import lax
from jax.sharding import PartitionSpec as P

D = 1024
HEAD_DIM = 128
CAP = 2
HD = 1024
EPSILON = 1e-05


def prefix_attention(group_queries, group_users, prefix_keys, prefix_values):
    group_size, block_width, half_width = group_queries.shape
    heads_here = half_width // HEAD_DIM
    safe_user = jnp.maximum(group_users, 0)
    user_keys = jnp.take(prefix_keys, safe_user, axis=0)
    user_values = jnp.take(prefix_values, safe_user, axis=0)
    query_heads = group_queries.reshape(group_size, block_width, heads_here, HEAD_DIM)
    key_heads = user_keys.reshape(group_size, -1, heads_here, HEAD_DIM)
    value_heads = user_values.reshape(group_size, -1, heads_here, HEAD_DIM)
    raw_scores = jnp.einsum(
        "gqhd,gkhd->ghqk", query_heads, key_heads, preferred_element_type=jnp.float32
    ) * HEAD_DIM ** (-0.5)
    weights = jax.nn.silu(raw_scores).astype(jnp.bfloat16)
    summed = jnp.einsum("ghqk,gkhd->gqhd", weights, value_heads, preferred_element_type=jnp.float32)
    return summed.reshape(group_size, block_width, half_width).astype(jnp.bfloat16)


def local(
    items,
    block_owner,
    block_user,
    block_fill,
    prefix_keys,
    prefix_values,
    w_in,
    attn_gain,
    w_o,
    mlp_gain,
    w_one,
    w_two,
):
    blocks, block_width, model_width = items.shape
    row_count = blocks * block_width
    half_width = w_in.shape[2]
    heads_here = half_width // HEAD_DIM
    peer_count = lax.axis_size("users")
    slot_count = peer_count * CAP
    score_scale = HEAD_DIM ** (-0.5)
    flat_items = items.reshape(row_count, model_width)
    projected = jnp.einsum(
        "rk,pkc->prc",
        flat_items,
        lax.all_gather(w_in, "routers", axis=1, tiled=True),
        preferred_element_type=jnp.float32,
    )
    activated = jax.nn.silu(projected)
    queries = activated[0].astype(jnp.bfloat16)
    target = block_owner[:, 0]
    earlier = lax.broadcasted_iota(jnp.int32, (blocks, blocks), 1) < lax.broadcasted_iota(
        jnp.int32, (blocks, blocks), 0
    )
    same_target = target[:, None] == target[None, :]
    dest_rank = jnp.sum((same_target & earlier).astype(jnp.int32), axis=1)
    position = target * CAP + dest_rank
    selector = lax.broadcasted_iota(jnp.int32, (slot_count, blocks), 0) == position[None, :]
    block_queries = queries.reshape(blocks, block_width * half_width)
    outgoing = jnp.dot(
        selector.astype(jnp.bfloat16), block_queries, preferred_element_type=jnp.float32
    ).astype(jnp.bfloat16)
    outgoing = outgoing.reshape(peer_count, CAP, block_width, half_width)
    slot_user = jnp.sum(jnp.where(selector, block_user[None, :] + 1, 0), axis=1) - 1
    slot_user = slot_user.reshape(peer_count, CAP)
    arrived = lax.all_to_all(outgoing, "users", split_axis=0, concat_axis=0, tiled=True)
    arrived_users = lax.all_to_all(slot_user, "users", split_axis=0, concat_axis=0, tiled=True)
    sources, per_source = arrived_users.shape
    total_slots = sources * per_source
    flat_queries = arrived.reshape(total_slots, block_width, half_width)
    flat_users = arrived_users.reshape(total_slots)
    packing = jnp.argsort((flat_users < 0).astype(jnp.int32), stable=True)
    used_slots = jnp.sum((flat_users >= 0).astype(jnp.int32))
    packed_queries = jnp.take(flat_queries, packing, axis=0)
    packed_users = jnp.take(flat_users, packing, axis=0)
    needed = (used_slots + 3) // 4

    def attend_group(group_index, buffer):
        first_slot = group_index * 4
        group_queries = lax.dynamic_slice_in_dim(packed_queries, first_slot, 4, 0)
        group_users = lax.dynamic_slice_in_dim(packed_users, first_slot, 4, 0)
        result = prefix_attention(group_queries, group_users, prefix_keys, prefix_values)
        return lax.dynamic_update_slice_in_dim(buffer, result, first_slot, 0)

    packed_out = lax.fori_loop(
        0, needed, attend_group, jnp.zeros((total_slots, block_width, half_width), jnp.bfloat16)
    )
    inverse = jnp.argsort(packing)
    attended_slots = jnp.take(packed_out, inverse, axis=0)
    returned = lax.all_to_all(
        attended_slots.reshape(sources, per_source, block_width, half_width),
        "users",
        split_axis=0,
        concat_axis=0,
        tiled=True,
    )
    prefix_part = jnp.take(returned.reshape(slot_count, block_width * half_width), position, axis=0)
    prefix_part = prefix_part.reshape(row_count, heads_here, HEAD_DIM).astype(jnp.float32)
    query_heads = queries.astype(jnp.float32).reshape(row_count, heads_here, HEAD_DIM)
    self_keys = activated[1].reshape(row_count, heads_here, HEAD_DIM)
    self_values = activated[2].reshape(row_count, heads_here, HEAD_DIM)
    own_term = (
        jax.nn.silu(jnp.sum(query_heads * self_keys, axis=-1) * score_scale)[..., None]
        * self_values
    )
    attended = (prefix_part + own_term).reshape(row_count, half_width)
    totals = lax.psum((jnp.sum(attended, axis=1), jnp.sum(attended * attended, axis=1)), "heads")
    row_mean = totals[0] / HD
    row_var = totals[1] / HD - row_mean * row_mean
    gated = (
        (attended - row_mean[:, None])
        * lax.rsqrt(row_var + EPSILON)[:, None]
        * attn_gain.astype(jnp.float32)
        * activated[3]
    ).astype(jnp.bfloat16)
    partial_out = jnp.dot(
        gated,
        lax.all_gather(w_o, "routers", axis=1, tiled=True),
        preferred_element_type=jnp.float32,
    )
    mixed = lax.psum(partial_out, "heads")
    residual = flat_items.astype(jnp.float32) + mixed
    row_scale = lax.rsqrt(jnp.sum(residual * residual, axis=1) / D + EPSILON)
    normed = (residual * row_scale[:, None] * mlp_gain.astype(jnp.float32)).astype(jnp.bfloat16)
    hidden = jax.nn.silu(jnp.dot(normed, w_one, preferred_element_type=jnp.float32)).astype(
        jnp.bfloat16
    )
    block_scores = jnp.dot(hidden, w_two, preferred_element_type=jnp.float32).reshape(
        blocks, block_width
    )
    is_valid = lax.broadcasted_iota(jnp.int32, (blocks, block_width), 1) < block_fill[:, None]
    return jnp.where(is_valid, block_scores, jnp.zeros_like(block_scores))


def solution(mesh):
    placed = (
        P(("groups", "users", "routers"), None, None),
        P(("groups", "users", "routers"), None),
        P(("groups", "users", "routers")),
        P(("groups", "users", "routers")),
        P(("groups", "users"), None, "heads"),
        P(("groups", "users"), None, "heads"),
        P(None, "routers", "heads"),
        P("heads"),
        P("heads", "routers"),
        P(),
        P(),
        P(),
    )
    return jax.shard_map(
        local,
        mesh=mesh,
        in_specs=placed,
        out_specs=P(("groups", "users", "routers"), None),
        check_vma=False,
    )
```

profile of v0, /device:TPU:0, one launch (start us, length us, event | category | flops | bytes accessed | tf_op | source)
XLA Modules:
  0.0 166.5 jit_solution(10524344665358077682)
XLA Ops:
  6.5 4.2 %copy.36 = bf16[4,512,512]{1,2,0:T(8,128)(2,1)} copy(bf16[4,512,512]{2,1,0:T(8,128)(2,1)} %param.24) | data formatting | bytes 4194304 | tf_op args[6]
  10.8 0.0 all-gather.3.cloned.1.call-update
  10.8 0.6 copy-done.10
  11.4 0.2 convert_reduce_fusion
  11.6 0.0 copy-done.12
  11.6 0.1 select_reduce_fusion
  11.7 0.7 sub.21
  12.4 6.3 %all-to-all-start = ((s32[4,1,2]{2,1,0:T(1,128)}), s32[4,1,2]{2,1,0:T(1,128)S(1)}, u32[]{:S(2)}, u32[]{:S(2)}) async-start(s32[4,1,2]{2,1,0:T(1,128)} %bitcast.5), calls=%async_computation | async-start | bytes 4096 | tf_op jit(solution)/shard_map/all_to_all | solution.py:76
  18.7 0.7 all-gather.5.cloned.1.call-update
  19.4 4.8 %all-to-all-done = s32[4,1,2]{2,1,0:T(1,128)S(1)} async-done(((s32[4,1,2]{2,1,0:T(1,128)}), s32[4,1,2]{2,1,0:T(1,128)S(1)}, u32[]{:S(2)}, u32[]{:S(2)}) %all-to-all-start) | async-done | bytes 64 | tf_op jit(solution)/shard_map/all_to_all | solution.py:76
  24.2 0.5 broadcast.235
  24.7 1.3 fusion.40
  26.0 0.1 reshape.118
  26.1 1.0 sort.34
  27.1 43.4 %all-gather.3.cloned.1.call-done = bf16[4,1024,512]{1,2,0:T(8,128)(2,1)} async-done(((bf16[4,512,512]{1,2,0:T(8,128)(2,1)}), bf16[4,1024,512]{1,2,0:T(8,128)(2,1)}) %all-gather.3.cloned.1.call-update) | async-done | bytes 4194320 | tf_op jit(solution)/shard_map/all_gather | solution.py:55
  70.4 0.0 copy-done.7
  70.4 3.6 %bitcast_multiply_fusion = f32[4,256,512]{1,2,0:T(8,128)S(1)} fusion(bf16[4,1024,512]{1,2,0:T(8,128)(2,1)} %all-gather.3.cloned.1.call-done, bf16[256,1024,1]{1,0,2:T(8,128)(2,1)S(1)} %bitcast.106), kind=kOutput, calls=%fused_computation.28 | convolution fusion | flops 1075838976 | bytes 6815744 | tf_op jit(solution)/shard_map/rk,pkc->prc/dot_general | solution.py:52
  74.0 0.0 copy-start.5
  74.0 1.3 copy-done.5
  75.4 0.9 slice_multiply_fusion
  76.3 0.1 copy.37
  76.4 0.2 convert_element_type.76
  76.6 0.4 convolution_convert_fusion.1
  77.0 1.0 copy.43
  78.0 4.7 %all-to-all-start.1 = ((bf16[4,2,64,512]{3,2,1,0:T(8,128)(2,1)}), bf16[4,2,64,512]{3,2,1,0:T(8,128)(2,1)S(1)}, u32[]{:S(2)}, u32[]{:S(2)}) async-start(bf16[4,2,64,512]{3,2,1,0:T(8,128)(2,1)} %bitcast.27), calls=%async_computation.1 | async-start | bytes 1048576 | tf_op jit(solution)/shard_map/all_to_all | solution.py:75
  83.4 0.6 gather_fusion.2
  84.0 1.0 sort.35
  85.0 12.0 %all-to-all-done.1 = bf16[4,2,64,512]{3,2,1,0:T(8,128)(2,1)S(1)} async-done(((bf16[4,2,64,512]{3,2,1,0:T(8,128)(2,1)}), bf16[4,2,64,512]{3,2,1,0:T(8,128)(2,1)S(1)}, u32[]{:S(2)}, u32[]{:S(2)}) %all-to-all-start.1) | async-done | bytes 524320 | tf_op jit(solution)/shard_map/all_to_all | solution.py:75
  97.0 0.6 gather_fusion.4
  97.6 0.9 broadcast_select_fusion.1
  98.6 0.9 broadcast_in_dim.66
  99.4 6.1 %while.10 = (s32[]{:T(128)}, bf16[8,64,512]{2,1,0:T(8,128)(2,1)}, s32[]{:T(128)}, s32[8]{0:T(128)S(1)}, bf16[2,256,512]{2,1,0:T(8,128)(2,1)S(1)}, /*index=5*/bf1...) while((s32[]{:T(128)}, bf16[8,64,512]{2,1,0:T(8,128)(2,1)}, ...), condition=%wide.region_5.8_spmd, body=%wide.region_4.7_spmd.sunk | while | flops 136971280 | bytes 13635875 | solution.py:94
  99.4 0.1 broadcast_compare_fusion.2
  99.5 0.6 gather_fusion
  100.1 0.6 gather_fusion.1
  100.7 1.5 select_bitcast_fusion.3
  102.3 2.5 %fusion.55 = bf16[4,4,8,8,128]{4,3,2,1,0:T(8,128)(2,1)S(1)} fusion(bf16[4,32,4,8,128]{4,3,2,1,0:T(8,128)(2,1)} %get-tuple-element.135, bf16[4,32,4,8,128]{4,3,2,1,0:T(8,128)(2,1)} %get-tuple-element.136, bf16[8,64,512]{2,1,0:T(8,128)(2,1)} %get-tuple-element.164, s32[]{:T(128)S(6)} %select_n.93), kind=kOutput, calls=%fused_computation.8.clone.1 | convolution fusion | flops 135921664 | bytes 2621444 | tf_op jit(solution)/shard_map/while/body/ghqk,gkhd->gqhd/dot_general | solution.py:26
  104.8 0.7 bitcast_dynamic-update-slice_fusion.2
  105.5 1.7 %gather_fusion.5 = bf16[8,64,512]{2,1,0:T(8,128)(2,1)S(1)} fusion(bf16[8,64,512]{2,1,0:T(8,128)(2,1)} %get-tuple-element.174, s32[1024]{0:T(1024)S(1)} %pad_clamp_fusion.2), kind=kCustom, calls=%fused_computation.2.clone | custom fusion | bytes 1048608 | tf_op jit(solution)/shard_map/jit(_take)/gather | solution.py:98
  107.2 0.9 broadcast_select_fusion
  108.1 3.5 %all-to-all-start.2 = ((bf16[4,2,64,512]{3,2,1,0:T(8,128)(2,1)}), bf16[4,2,64,512]{3,2,1,0:T(8,128)(2,1)S(1)}, u32[]{:S(2)}, u32[]{:S(2)}) async-start(bf16[4,2,64,512]{3,2,1,0:T(8,128)(2,1)} %bitcast.9), calls=%async_computation.2 | async-start | bytes 1048576 | tf_op jit(solution)/shard_map/all_to_all | solution.py:99
  111.6 0.0 all-reduce.3.cloned.1.call-start
  111.7 0.1 broadcast_in_dim.63
  111.8 0.1 broadcast_in_dim.64
  111.9 13.7 %all-to-all-done.2 = bf16[4,2,64,512]{3,2,1,0:T(8,128)(2,1)S(1)} async-done(((bf16[4,2,64,512]{3,2,1,0:T(8,128)(2,1)}), bf16[4,2,64,512]{3,2,1,0:T(8,128)(2,1)S(1)}, u32[]{:S(2)}, u32[]{:S(2)}) %all-to-all-start.2) | async-done | bytes 524320 | tf_op jit(solution)/shard_map/all_to_all | solution.py:99
  125.6 0.3 copy.44
  125.9 0.0 copy-start.6
  125.9 0.8 gather_fusion.3
  126.7 0.2 gather.18
  126.9 0.1 copy.38
  127.1 0.5 copy-done.6
  127.5 0.1 fusion.39
  127.7 2.5 %all-reduce = (f32[256]{0:T(256)S(1)}, f32[256]{0:T(256)S(1)}) all-reduce(f32[256]{0:T(256)S(1)} %get-tuple-element.51, f32[256]{0:T(256)S(1)} %get-tuple-element.50), channel_id=1, replica_groups=mesh['groups'=2,'users'=4,'routers'=2,'heads'=2] {'heads'}, use_global_device_ids=true, to_apply=%region_11.14 | all-reduce | flops 512 | bytes 4096 | tf_op jit(solution)/shard_map/psum | solution.py:116
  130.1 0.0 all-gather.5.cloned.1.call-done
  130.2 0.0 copy-start.9
  130.2 0.0 copy-start.14
  130.2 2.8 %fusion.27 = f32[256,1024]{1,0:T(8,128)} fusion(bf16[512,1024]{1,0:T(8,128)(2,1)} %all-gather.5.cloned.1.call-done, f32[4,256,512]{1,2,0:T(8,128)S(1)} %copy-done.6, f32[256,512]{0,1:T(8,128)S(1)} %get-tuple-element.72, f32[512]{0:T(512)S(1)} %convert_element_type.80, f32[256]{0:T(256)S(1)} %get-tuple-element.82, f32[256]{0:T(256)S(1)} %get-tuple-element.81), kind=kOutput, calls=%fused_computation.50 | convolution fusion | flops 269090816 | bytes 3149824 | tf_op jit(solution)/shard_map/dot_general | solution.py:125
  133.0 0.0 all-reduce.3.cloned.1.call-update
  133.0 0.0 copy-start.13
  133.1 22.9 %all-reduce.3.cloned.1.call-done = f32[256,1024]{1,0:T(8,128)} async-done(((f32[256,1024]{1,0:T(8,128)}), f32[256,1024]{1,0:T(8,128)}) %all-reduce.3.cloned.1.call-update) | async-done | bytes 1048592 | tf_op jit(solution)/shard_map/psum | solution.py:130
  155.9 1.6 multiply_reduce_fusion
  157.5 1.7 %fusion.29 = f32[1,256]{1,0:T(1,128)S(1)} fusion(bf16[256,1]{0,1:T(2,128)(2,1)S(1)} %reshape.186, bf16[1024,256]{1,0:T(8,128)(2,1)S(1)} %copy-done, f32[256,1024]{1,0:T(8,128)} %all-reduce.3.cloned.1.call-done, bf16[256,1024]{1,0:T(8,128)(2,1)S(1)} %bitcast.107, f32[1024]{0:T(1024)S(1)} %convert_element_type.82, f32[256]{0:T(256)S(1)} %add_rsqrt_fusion), kind=kOutput, calls=%fused_computation.52 | convolution fusion | flops 135987200 | bytes 2103808 | tf_op jit(solution)/shard_map/dot_general | solution.py:137
  159.2 0.1 reshape.123
  159.3 0.7 fusion.35
  (43 shorter events, 0.2 us)
Async XLA Ops:
  6.5 151.0 %copy-start = (bf16[1024,256]{1,0:T(8,128)(2,1)S(1)}, bf16[1024,256]{1,0:T(8,128)(2,1)}, u32[]{:S(2)}) copy-start(bf16[1024,256]{1,0:T(8,128)(2,1)} %param.28) | copy-start | bytes 1572868
  6.5 63.9 %all-gather.3.cloned.1.call-start = ((), (), s32[]{:S(2)}) async-start(), calls=%async_computation.3 | async-start | bytes 6291456 | tf_op jit(solution)/shard_map/all_gather | solution.py:55
  10.7 0.7 copy-start.10
  10.7 0.8 copy-start.12
  10.8 59.7 %copy-start.7 = (bf16[4,64,1024]{2,1,0:T(8,128)(2,1)S(1)}, bf16[4,64,1024]{2,1,0:T(8,128)(2,1)}, u32[]{:S(2)}) copy-start(bf16[4,64,1024]{2,1,0:T(8,128)(2,1)} %param.18) | copy-start | bytes 1572868
  12.4 11.8 %all-to-all-start = ((s32[4,1,2]{2,1,0:T(1,128)}), s32[4,1,2]{2,1,0:T(1,128)S(1)}, u32[]{:S(2)}, u32[]{:S(2)}) async-start(s32[4,1,2]{2,1,0:T(1,128)} %bitcast.5), calls=%async_computation | async-start | bytes 4096 | tf_op jit(solution)/shard_map/all_to_all | solution.py:76
  18.7 111.4 %all-gather.5.cloned.1.call-start = ((), (), s32[]{:S(2)}) async-start(), calls=%async_computation.4 | async-start | bytes 1572864 | tf_op jit(solution)/shard_map/all_gather | solution.py:127
  74.0 1.4 copy-start.5
  78.0 21.4 %copy-start.1 = (bf16[2,256,512]{2,1,0:T(8,128)(2,1)S(1)}, bf16[2,256,512]{2,1,0:T(8,128)(2,1)}, u32[]{:S(2)}) copy-start(bf16[2,256,512]{2,1,0:T(8,128)(2,1)} %param.23) | copy-start | bytes 1572868
  78.0 21.4 %copy-start.2 = (bf16[2,256,512]{2,1,0:T(8,128)(2,1)S(1)}, bf16[2,256,512]{2,1,0:T(8,128)(2,1)}, u32[]{:S(2)}) copy-start(bf16[2,256,512]{2,1,0:T(8,128)(2,1)} %param.22) | copy-start | bytes 1572868
  78.0 19.1 %all-to-all-start.1 = ((bf16[4,2,64,512]{3,2,1,0:T(8,128)(2,1)}), bf16[4,2,64,512]{3,2,1,0:T(8,128)(2,1)S(1)}, u32[]{:S(2)}, u32[]{:S(2)}) async-start(bf16[4,2,64,512]{3,2,1,0:T(8,128)(2,1)} %bitcast.27), calls=%async_computation.1 | async-start | bytes 1048576 | tf_op jit(solution)/shard_map/all_to_all | solution.py:75
  102.3 3.2 %copy-start.3 = (bf16[2,256,512]{2,1,0:T(8,128)(2,1)S(1)}, bf16[2,256,512]{2,1,0:T(8,128)(2,1)}, u32[]{:S(2)}) copy-start(bf16[2,256,512]{2,1,0:T(8,128)(2,1)} %get-tuple-element.184) | copy-start | bytes 1572868 | tf_op jit(solution)/shard_map/while
  105.5 6.3 %copy-start.11 = (bf16[512]{0:T(512)(128)(2,1)S(1)}, bf16[512]{0:T(512)(128)(2,1)}, u32[]{:S(2)}) copy-start(bf16[512]{0:T(512)(128)(2,1)} %param.25) | copy-start | bytes 3076
  105.5 6.3 %copy-start.4 = (f32[1,256,512]{1,2,0:T(8,128)S(1)}, f32[1,256,512]{1,2,0:T(8,128)}, u32[]{:S(2)}) copy-start(f32[1,256,512]{1,2,0:T(8,128)} %get-tuple-element.77) | copy-start | bytes 1572868
  108.1 17.5 %all-to-all-start.2 = ((bf16[4,2,64,512]{3,2,1,0:T(8,128)(2,1)}), bf16[4,2,64,512]{3,2,1,0:T(8,128)(2,1)S(1)}, u32[]{:S(2)}, u32[]{:S(2)}) async-start(bf16[4,2,64,512]{3,2,1,0:T(8,128)(2,1)} %bitcast.9), calls=%async_computation.2 | async-start | bytes 1048576 | tf_op jit(solution)/shard_map/all_to_all | solution.py:99
  111.6 44.3 %all-reduce.3.cloned.1.call-start = ((), (), s32[]{:S(2)}) async-start(), calls=%async_computation.5 | async-start | bytes 2097152 | tf_op jit(solution)/shard_map/psum | solution.py:130
  125.9 1.6 copy-start.6
  130.2 2.8 %copy-start.9 = (bf16[1024]{0:T(1024)(128)(2,1)S(1)}, bf16[1024]{0:T(1024)(128)(2,1)}, u32[]{:S(2)}) copy-start(bf16[1024]{0:T(1024)(128)(2,1)} %param.27) | copy-start | bytes 6148
  130.2 2.9 %copy-start.14 = (bf16[256]{0:T(256)(128)(2,1)S(1)}, bf16[256]{0:T(256)(128)(2,1)}, u32[]{:S(2)}) copy-start(bf16[256]{0:T(256)(128)(2,1)} %param.29) | copy-start | bytes 1540
  133.0 24.5 %copy-start.8 = (bf16[4,64,1024]{2,1,0:T(8,128)(2,1)S(1)}, bf16[4,64,1024]{2,1,0:T(8,128)(2,1)}, u32[]{:S(2)}) copy-start(bf16[4,64,1024]{2,1,0:T(8,128)(2,1)} %param.18) | copy-start | bytes 1572868
  133.0 26.3 %copy-start.13 = (s32[4]{0:T(128)S(1)}, s32[4]{0:T(128)}, u32[]{:S(2)}) copy-start(s32[4]{0:T(128)} %param.21) | copy-start | bytes 52
Sparse Core Ops, SparseCore 0:
  10.9 59.4 all-gather.2
  72.0 21.2 all-gather.4
  133.1 22.7 all-reduce.2
where the time goes:
time: 167 us; the launch traced here: 166 us
  waiting for transfers between devices  97.4 us (58%)
  local copies, waits for them, and re-layouts  16.6 us (10%)
  starting transfers between devices  14.6 us (9%)
  between operations  14 us (8%)
  matrix products  11 us (7%)
  other arithmetic  10.4 us (6%)
  blocking collectives  2.46 us (1%)
    all_gather x1, waiting for transfers between devices, local(): lax.all_gather(w_in, 'routers', axis=1, tiled=True)  43.4 us
    psum x1, waiting for transfers between devices, local(): mixed = lax.psum(partial_out, 'heads')  22.9 us
    all_to_all x1, waiting for transfers between devices, local(): lax.all_to_all(attended_slots.reshape(sources, per_source, block_width, h...  13.7 us
    all_to_all x1, waiting for transfers between devices, local(): lax.all_to_all(outgoing, 'users', split_axis=0, concat_axis=0, tiled=True)  12 us
    unnamed x32, local copies, waits for them, and re-layouts  7.95 us
    all_to_all x1, starting transfers between devices, local(): lax.all_to_all(slot_user, 'users', split_axis=0, concat_axis=0, tiled=True)  6.35 us
    all_to_all x1, waiting for transfers between devices, local(): lax.all_to_all(slot_user, 'users', split_axis=0, concat_axis=0, tiled=True)  4.76 us
    all_to_all x1, starting transfers between devices, local(): lax.all_to_all(outgoing, 'users', split_axis=0, concat_axis=0, tiled=True)  4.73 us
  transfers between devices with their start and end apart: 6, of which 5 were waited for; matrix products, arithmetic and copies ran while one was open for 15% of the time, Pallas kernels for 0%

commit v1 on v0

--- a/solution.py
+++ b/solution.py
@@ -127,7 +127,7 @@
         lax.all_gather(w_o, "routers", axis=1, tiled=True),
         preferred_element_type=jnp.float32,
     )
-    mixed = lax.psum(partial_out, "heads")
+    mixed = jnp.sum(lax.all_gather(partial_out, "heads"), axis=0)
     residual = flat_items.astype(jnp.float32) + mixed
     row_scale = lax.rsqrt(jnp.sum(residual * residual, axis=1) / D + EPSILON)
     normed = (residual * row_scale[:, None] * mlp_gain.astype(jnp.float32)).astype(jnp.bfloat16)

time: 167 us -> 158 us (0.946)
  waiting for transfers between devices: 97.4 us -> 88.6 us
    psum x1 -> x0, waiting for transfers between devices: 22.9 us -> none  [local(): mixed = lax.psum(partial_out, 'heads')]
    all_gather x0 -> x1, waiting for transfers between devices: none -> 14 us  [local(): mixed = jnp.sum(lax.all_gather(partial_out, 'heads'), axis=0)]
    reduce_sum x0 -> x1, other arithmetic: none -> 1.85 us  [local(): mixed = jnp.sum(lax.all_gather(partial_out, 'heads'), axis=0)]
  transfers between devices with their start and end apart: 6 -> 6, of which waited for: 5 -> 5; matrix products, arithmetic and copies ran while one was open for 15% -> 16% of each run, Pallas kernels for 0% -> 0%
where the time goes in v1:
time: 158 us; the launch traced here: 157 us
  waiting for transfers between devices  88.6 us (56%)
  local copies, waits for them, and re-layouts  16.7 us (11%)
  starting transfers between devices  14.6 us (9%)
  between operations  14 us (9%)
  other arithmetic  10.9 us (7%)
  matrix products  9.75 us (6%)
  blocking collectives  2.46 us (2%)
    all_gather x1, waiting for transfers between devices, local(): lax.all_gather(w_in, 'routers', axis=1, tiled=True)  43.4 us
    all_gather x1, waiting for transfers between devices, local(): mixed = jnp.sum(lax.all_gather(partial_out, 'heads'), axis=0)  14 us
    all_to_all x1, waiting for transfers between devices, local(): lax.all_to_all(attended_slots.reshape(sources, per_source, block_width, h...  13.7 us
    all_to_all x1, waiting for transfers between devices, local(): lax.all_to_all(outgoing, 'users', split_axis=0, concat_axis=0, tiled=True)  12 us
    unnamed x32, local copies, waits for them, and re-layouts  7.95 us
    all_to_all x1, starting transfers between devices, local(): lax.all_to_all(slot_user, 'users', split_axis=0, concat_axis=0, tiled=True)  6.35 us
    all_to_all x1, waiting for transfers between devices, local(): lax.all_to_all(slot_user, 'users', split_axis=0, concat_axis=0, tiled=True)  4.76 us
    all_to_all x1, starting transfers between devices, local(): lax.all_to_all(outgoing, 'users', split_axis=0, concat_axis=0, tiled=True)  4.73 us
  transfers between devices with their start and end apart: 6, of which 5 were waited for; matrix products, arithmetic and copies ran while one was open for 16% of the time, Pallas kernels for 0%

profile of v1, /device:TPU:0, one launch (start us, length us, event | category | flops | bytes accessed | tf_op | source)
XLA Modules:
  0.0 157.0 jit_solution(7574882432108518667)
XLA Ops:
  6.5 4.2 %copy.36 = bf16[4,512,512]{1,2,0:T(8,128)(2,1)} copy(bf16[4,512,512]{2,1,0:T(8,128)(2,1)} %param.24) | data formatting | bytes 4194304 | tf_op args[6]
  10.8 0.0 all-gather.5.cloned.1.call-update
  10.8 0.6 copy-done.10
  11.4 0.2 convert_reduce_fusion
  11.6 0.0 copy-done.12
  11.6 0.1 select_reduce_fusion
  11.7 0.7 sub.21
  12.4 6.3 %all-to-all-start = ((s32[4,1,2]{2,1,0:T(1,128)}), s32[4,1,2]{2,1,0:T(1,128)S(1)}, u32[]{:S(2)}, u32[]{:S(2)}) async-start(s32[4,1,2]{2,1,0:T(1,128)} %bitcast.5), calls=%async_computation | async-start | bytes 4096 | tf_op jit(solution)/shard_map/all_to_all | solution.py:76
  18.7 0.7 all-gather.7.cloned.1.call-update
  19.4 4.8 %all-to-all-done = s32[4,1,2]{2,1,0:T(1,128)S(1)} async-done(((s32[4,1,2]{2,1,0:T(1,128)}), s32[4,1,2]{2,1,0:T(1,128)S(1)}, u32[]{:S(2)}, u32[]{:S(2)}) %all-to-all-start) | async-done | bytes 64 | tf_op jit(solution)/shard_map/all_to_all | solution.py:76
  24.2 0.5 broadcast.245
  24.7 1.3 fusion.40
  26.0 0.1 reshape.128
  26.1 1.0 sort.34
  27.1 43.4 %all-gather.5.cloned.1.call-done = bf16[4,1024,512]{1,2,0:T(8,128)(2,1)} async-done(((bf16[4,512,512]{1,2,0:T(8,128)(2,1)}), bf16[4,1024,512]{1,2,0:T(8,128)(2,1)}) %all-gather.5.cloned.1.call-update) | async-done | bytes 4194320 | tf_op jit(solution)/shard_map/all_gather | solution.py:55
  70.4 0.0 copy-done.7
  70.4 3.6 %bitcast_multiply_fusion = f32[4,256,512]{1,2,0:T(8,128)S(1)} fusion(bf16[4,1024,512]{1,2,0:T(8,128)(2,1)} %all-gather.5.cloned.1.call-done, bf16[256,1024,1]{1,0,2:T(8,128)(2,1)S(1)} %bitcast.109), kind=kOutput, calls=%fused_computation.28 | convolution fusion | flops 1075838976 | bytes 6815744 | tf_op jit(solution)/shard_map/rk,pkc->prc/dot_general | solution.py:52
  74.0 1.3 copy-done.5
  75.4 0.9 slice_multiply_fusion
  76.3 0.1 copy.37
  76.4 0.2 convert_element_type.79
  76.6 0.4 convolution_convert_fusion.1
  77.0 1.0 copy.43
  78.0 4.7 %all-to-all-start.1 = ((bf16[4,2,64,512]{3,2,1,0:T(8,128)(2,1)}), bf16[4,2,64,512]{3,2,1,0:T(8,128)(2,1)S(1)}, u32[]{:S(2)}, u32[]{:S(2)}) async-start(bf16[4,2,64,512]{3,2,1,0:T(8,128)(2,1)} %bitcast.29), calls=%async_computation.1 | async-start | bytes 1048576 | tf_op jit(solution)/shard_map/all_to_all | solution.py:75
  83.4 0.6 gather_fusion.2
  84.0 1.0 sort.35
  85.0 12.0 %all-to-all-done.1 = bf16[4,2,64,512]{3,2,1,0:T(8,128)(2,1)S(1)} async-done(((bf16[4,2,64,512]{3,2,1,0:T(8,128)(2,1)}), bf16[4,2,64,512]{3,2,1,0:T(8,128)(2,1)S(1)}, u32[]{:S(2)}, u32[]{:S(2)}) %all-to-all-start.1) | async-done | bytes 524320 | tf_op jit(solution)/shard_map/all_to_all | solution.py:75
  97.0 0.6 gather_fusion.4
  97.6 0.9 broadcast_select_fusion.1
  98.6 0.9 broadcast_in_dim.66
  99.4 6.1 %while.10 = (s32[]{:T(128)}, bf16[8,64,512]{2,1,0:T(8,128)(2,1)}, s32[]{:T(128)}, s32[8]{0:T(128)S(1)}, bf16[2,256,512]{2,1,0:T(8,128)(2,1)S(1)}, /*index=5*/bf1...) while((s32[]{:T(128)}, bf16[8,64,512]{2,1,0:T(8,128)(2,1)}, ...), condition=%wide.region_5.8_spmd, body=%wide.region_4.7_spmd.sunk | while | flops 136971280 | bytes 13635875 | solution.py:94
  99.4 0.1 broadcast_compare_fusion.2
  99.5 0.6 gather_fusion
  100.1 0.6 gather_fusion.1
  100.7 1.5 select_bitcast_fusion.3
  102.3 2.5 %fusion.55 = bf16[4,4,8,8,128]{4,3,2,1,0:T(8,128)(2,1)S(1)} fusion(bf16[4,32,4,8,128]{4,3,2,1,0:T(8,128)(2,1)} %get-tuple-element.135, bf16[4,32,4,8,128]{4,3,2,1,0:T(8,128)(2,1)} %get-tuple-element.136, bf16[8,64,512]{2,1,0:T(8,128)(2,1)} %get-tuple-element.164, s32[]{:T(128)S(6)} %select_n.93), kind=kOutput, calls=%fused_computation.8.clone.1 | convolution fusion | flops 135921664 | bytes 2621444 | tf_op jit(solution)/shard_map/while/body/ghqk,gkhd->gqhd/dot_general | solution.py:26
  104.8 0.7 bitcast_dynamic-update-slice_fusion.2
  105.5 1.7 %gather_fusion.5 = bf16[8,64,512]{2,1,0:T(8,128)(2,1)S(1)} fusion(bf16[8,64,512]{2,1,0:T(8,128)(2,1)} %get-tuple-element.174, s32[1024]{0:T(1024)S(1)} %pad_clamp_fusion.2), kind=kCustom, calls=%fused_computation.2.clone | custom fusion | bytes 1048608 | tf_op jit(solution)/shard_map/jit(_take)/gather | solution.py:98
  107.2 0.9 broadcast_select_fusion
  108.1 3.5 %all-to-all-start.2 = ((bf16[4,2,64,512]{3,2,1,0:T(8,128)(2,1)}), bf16[4,2,64,512]{3,2,1,0:T(8,128)(2,1)S(1)}, u32[]{:S(2)}, u32[]{:S(2)}) async-start(bf16[4,2,64,512]{3,2,1,0:T(8,128)(2,1)} %bitcast.9), calls=%async_computation.2 | async-start | bytes 1048576 | tf_op jit(solution)/shard_map/all_to_all | solution.py:99
  111.6 0.0 all-gather.9.cloned.1.call-start
  111.7 0.1 broadcast_in_dim.63
  111.8 0.1 broadcast_in_dim.64
  111.9 13.7 %all-to-all-done.2 = bf16[4,2,64,512]{3,2,1,0:T(8,128)(2,1)S(1)} async-done(((bf16[4,2,64,512]{3,2,1,0:T(8,128)(2,1)}), bf16[4,2,64,512]{3,2,1,0:T(8,128)(2,1)S(1)}, u32[]{:S(2)}, u32[]{:S(2)}) %all-to-all-start.2) | async-done | bytes 524320 | tf_op jit(solution)/shard_map/all_to_all | solution.py:99
  125.6 0.3 copy.44
  125.9 0.8 gather_fusion.3
  126.7 0.2 gather.18
  126.9 0.1 copy.38
  127.1 0.5 copy-done.6
  127.5 0.1 fusion.39
  127.7 2.5 %all-reduce = (f32[256]{0:T(256)S(1)}, f32[256]{0:T(256)S(1)}) all-reduce(f32[256]{0:T(256)S(1)} %get-tuple-element.51, f32[256]{0:T(256)S(1)} %get-tuple-element.50), channel_id=1, replica_groups=mesh['groups'=2,'users'=4,'routers'=2,'heads'=2] {'heads'}, use_global_device_ids=true, to_apply=%region_11.14 | all-reduce | flops 512 | bytes 4096 | tf_op jit(solution)/shard_map/psum | solution.py:116
  130.1 0.0 all-gather.7.cloned.1.call-done
  130.2 0.0 copy-start.9
  130.2 0.0 copy-start.14
  130.2 2.8 %fusion.27 = f32[256,1024]{1,0:T(8,128)} fusion(bf16[512,1024]{1,0:T(8,128)(2,1)} %all-gather.7.cloned.1.call-done, f32[4,256,512]{1,2,0:T(8,128)S(1)} %copy-done.6, f32[256,512]{0,1:T(8,128)S(1)} %get-tuple-element.72, f32[512]{0:T(512)S(1)} %convert_element_type.83, f32[256]{0:T(256)S(1)} %get-tuple-element.82, f32[256]{0:T(256)S(1)} %get-tuple-element.81), kind=kOutput, calls=%fused_computation.49 | convolution fusion | flops 269090816 | bytes 3149824 | tf_op jit(solution)/shard_map/dot_general | solution.py:125
  133.0 0.0 all-gather.9.cloned.1.call-update
  133.0 14.0 %all-gather.9.cloned.1.call-done = f32[512,1024]{1,0:T(8,128)} async-done(((f32[256,1024]{1,0:T(8,128)}), f32[512,1024]{1,0:T(8,128)}) %all-gather.9.cloned.1.call-update) | async-done | bytes 2097168 | tf_op jit(solution)/shard_map/all_gather | solution.py:130
  147.0 1.8 %reduce_sum.83 = f32[256,1024]{1,0:T(8,128)S(1)} reduce(f32[2,256,1024]{2,1,0:T(8,128)} %bitcast.105, f32[]{:T(128)} %constant.102.clone.1), dimensions={0}, to_apply=%region_12.15 | reduce | flops 262144 | bytes 3145732 | tf_op jit(solution)/shard_map/reduce_sum | solution.py:130
  148.9 0.0 copy-start.13
  148.9 0.2 multiply_reduce_fusion
  149.1 0.1 rsqrt.15
  149.2 0.5 fusion.29
  149.7 0.1 reshape.133
  149.8 0.7 fusion.35
  (45 shorter events, 0.2 us)
Async XLA Ops:
  6.5 142.7 %copy-start = (bf16[1024,256]{1,0:T(8,128)(2,1)S(1)}, bf16[1024,256]{1,0:T(8,128)(2,1)}, u32[]{:S(2)}) copy-start(bf16[1024,256]{1,0:T(8,128)(2,1)} %param.28) | copy-start | bytes 1572868
  6.5 63.9 %all-gather.5.cloned.1.call-start = ((), (), s32[]{:S(2)}) async-start(), calls=%async_computation.3 | async-start | bytes 6291456 | tf_op jit(solution)/shard_map/all_gather | solution.py:55
  10.7 0.7 copy-start.10
  10.7 0.8 copy-start.12
  10.8 59.7 %copy-start.7 = (bf16[4,64,1024]{2,1,0:T(8,128)(2,1)S(1)}, bf16[4,64,1024]{2,1,0:T(8,128)(2,1)}, u32[]{:S(2)}) copy-start(bf16[4,64,1024]{2,1,0:T(8,128)(2,1)} %param.18) | copy-start | bytes 1572868
  12.4 11.8 %all-to-all-start = ((s32[4,1,2]{2,1,0:T(1,128)}), s32[4,1,2]{2,1,0:T(1,128)S(1)}, u32[]{:S(2)}, u32[]{:S(2)}) async-start(s32[4,1,2]{2,1,0:T(1,128)} %bitcast.5), calls=%async_computation | async-start | bytes 4096 | tf_op jit(solution)/shard_map/all_to_all | solution.py:76
  18.7 111.4 %all-gather.7.cloned.1.call-start = ((), (), s32[]{:S(2)}) async-start(), calls=%async_computation.4 | async-start | bytes 1572864 | tf_op jit(solution)/shard_map/all_gather | solution.py:127
  74.0 1.4 copy-start.5
  78.0 21.4 %copy-start.1 = (bf16[2,256,512]{2,1,0:T(8,128)(2,1)S(1)}, bf16[2,256,512]{2,1,0:T(8,128)(2,1)}, u32[]{:S(2)}) copy-start(bf16[2,256,512]{2,1,0:T(8,128)(2,1)} %param.23) | copy-start | bytes 1572868
  78.0 21.4 %copy-start.2 = (bf16[2,256,512]{2,1,0:T(8,128)(2,1)S(1)}, bf16[2,256,512]{2,1,0:T(8,128)(2,1)}, u32[]{:S(2)}) copy-start(bf16[2,256,512]{2,1,0:T(8,128)(2,1)} %param.22) | copy-start | bytes 1572868
  78.0 19.1 %all-to-all-start.1 = ((bf16[4,2,64,512]{3,2,1,0:T(8,128)(2,1)}), bf16[4,2,64,512]{3,2,1,0:T(8,128)(2,1)S(1)}, u32[]{:S(2)}, u32[]{:S(2)}) async-start(bf16[4,2,64,512]{3,2,1,0:T(8,128)(2,1)} %bitcast.29), calls=%async_computation.1 | async-start | bytes 1048576 | tf_op jit(solution)/shard_map/all_to_all | solution.py:75
  102.3 3.2 %copy-start.3 = (bf16[2,256,512]{2,1,0:T(8,128)(2,1)S(1)}, bf16[2,256,512]{2,1,0:T(8,128)(2,1)}, u32[]{:S(2)}) copy-start(bf16[2,256,512]{2,1,0:T(8,128)(2,1)} %get-tuple-element.184) | copy-start | bytes 1572868 | tf_op jit(solution)/shard_map/while
  105.5 6.3 %copy-start.11 = (bf16[512]{0:T(512)(128)(2,1)S(1)}, bf16[512]{0:T(512)(128)(2,1)}, u32[]{:S(2)}) copy-start(bf16[512]{0:T(512)(128)(2,1)} %param.25) | copy-start | bytes 3076
  105.5 6.3 %copy-start.4 = (f32[1,256,512]{1,2,0:T(8,128)S(1)}, f32[1,256,512]{1,2,0:T(8,128)}, u32[]{:S(2)}) copy-start(f32[1,256,512]{1,2,0:T(8,128)} %get-tuple-element.77) | copy-start | bytes 1572868
  108.1 17.5 %all-to-all-start.2 = ((bf16[4,2,64,512]{3,2,1,0:T(8,128)(2,1)}), bf16[4,2,64,512]{3,2,1,0:T(8,128)(2,1)S(1)}, u32[]{:S(2)}, u32[]{:S(2)}) async-start(bf16[4,2,64,512]{3,2,1,0:T(8,128)(2,1)} %bitcast.9), calls=%async_computation.2 | async-start | bytes 1048576 | tf_op jit(solution)/shard_map/all_to_all | solution.py:99
  111.6 35.4 %all-gather.9.cloned.1.call-start = ((), (), s32[]{:S(2)}) async-start(), calls=%async_computation.5 | async-start | bytes 3145728 | tf_op jit(solution)/shard_map/all_gather | solution.py:130
  125.9 1.6 %copy-start.6 = (f32[4,256,512]{1,2,0:T(8,128)S(1)}, f32[4,256,512]{1,2,0:T(8,128)}, u32[]{:S(2)}) copy-start(f32[4,256,512]{1,2,0:T(8,128)} %copy-done.5) | copy-start | bytes 6291460
  130.2 2.8 %copy-start.9 = (bf16[1024]{0:T(1024)(128)(2,1)S(1)}, bf16[1024]{0:T(1024)(128)(2,1)}, u32[]{:S(2)}) copy-start(bf16[1024]{0:T(1024)(128)(2,1)} %param.27) | copy-start | bytes 6148
  130.2 2.8 %copy-start.14 = (bf16[256]{0:T(256)(128)(2,1)S(1)}, bf16[256]{0:T(256)(128)(2,1)}, u32[]{:S(2)}) copy-start(bf16[256]{0:T(256)(128)(2,1)} %param.29) | copy-start | bytes 1540
  133.0 15.9 %copy-start.8 = (bf16[4,64,1024]{2,1,0:T(8,128)(2,1)S(1)}, bf16[4,64,1024]{2,1,0:T(8,128)(2,1)}, u32[]{:S(2)}) copy-start(bf16[4,64,1024]{2,1,0:T(8,128)(2,1)} %param.18) | copy-start | bytes 1572868
  148.9 0.9 copy-start.13
Sparse Core Ops, SparseCore 0:
  10.9 59.4 all-gather.4
  72.0 21.2 all-gather.6
  133.1 13.8 all-gather.8
